TPU v7x, 256 devices: a whole 4x4x8 slice. The times are simulated.
256 devices in a mesh: seq: 2 (over core), chan: 16 (over y, x), batch: 8 (over z).
Axes of the slice: x: 4, y: 4, z: 8, core: 2. Of those that a mesh axis runs over, the one named last changes fastest.
Arguments:
- ssm_input: bfloat16 [16384, 4096], P(('batch', 'seq'), 'chan'), parts along dimension 0, may hold values from -6 to 6
- gate_z: bfloat16 [16384, 4096], P(('batch', 'seq'), 'chan'), parts along dimension 0, may hold values from -6 to 6
- proj_forward: bfloat16 [2, 16384, 128], P(None, ('batch', 'seq')), parts along dimension 1, may hold values from -2 to 2
- proj_backward: bfloat16 [2, 16384, 128], P(None, ('batch', 'seq')), parts along dimension 1, may hold values from -2 to 2
- step_raw: float32 [2, 64, 16384], P(None, 'chan', ('batch', 'seq')), parts along dimension 2, may hold values from -3 to 3
- head_params: float32 [2, 2, 64], P(None, None, 'chan'), may hold values from -4 to 1, as said below
- skip_gain: float32 [64], P('chan'), may hold values from 0.25 to 2
- norm_gain: float32 [4096], P('chan'), may hold values from 0.5 to 1.5
- out_weight: bfloat16 [4096, 2048], P(None, 'chan'), may hold values from -0.09375 to 0.09375
Outputs:
- mixed: bfloat16 [16384, 2048], P(('batch', 'seq'), 'chan'), parts along dimension 0
There are 8 independent parts, one for each index of `batch`. A program takes and returns all parts, laid end to end along the dimension named above; an argument that names none is the same for every part. Nothing has to cross between parts.
Inputs may be any that keep to these rules, and one draw needn't show every extreme that they name: `head_params`: index 0 of the second dimension holds positive decay rates, index 1 time-step biases.
All inputs are finite; a program needn't handle non-finite values.
Results may differ from a plain program's by a relative error of at most 0.0085.
Values may be sent and summed in bfloat16 or wider, within the bound.
A program may use at most 128 MiB of HBM per device.

v0:
```python
import jax
import jax.numpy as jnp
from jax import lax
from jax.sharding import PartitionSpec as P

SPAN = 256
INNER = 4096


def sent_together(arrays, axis, dim, along):
    columns = [a.reshape(*a.shape[:along], -1) for a in arrays]
    both = jnp.concatenate(columns, axis=along)
    whole, at, done = (lax.all_gather(both, axis, axis=dim, tiled=True), 0, [])
    for a, column in zip(arrays, columns):
        slab = whole[..., at : at + column.shape[along]]
        done.append(slab.reshape(*slab.shape[:along], *a.shape[along:]))
        at += column.shape[along]
    return tuple(done)


def copy_for_each(value, axis):
    copies = jnp.broadcast_to(value, (lax.axis_size(axis), *value.shape))
    return lax.all_to_all(copies, axis, split_axis=0, concat_axis=0, tiled=True)


def taken_together(value, axis):
    everything = copy_for_each(value, axis)
    return jnp.sum(everything, axis=0)


def local_scan(blocks_x, b_rows, c_rows, steps_here, decay_rates):
    cumlog = jnp.cumsum(-decay_rates[None, :, None] * steps_here, axis=2)
    scores = jnp.einsum("cqn,csn->cqs", c_rows, b_rows, preferred_element_type=jnp.float32)
    lower_mask = jnp.tril(jnp.ones((SPAN, SPAN), dtype=bool))
    log_gaps = cumlog[:, :, :, None] - cumlog[:, :, None, :]
    decays = jnp.where(lower_mask, jnp.exp(jnp.where(lower_mask, log_gaps, 0.0)), 0.0)
    weights = (scores[:, None] * decays * steps_here[:, :, None, :]).astype(jnp.bfloat16)
    intra_out = jnp.einsum("chts,cshp->cthp", weights, blocks_x, preferred_element_type=jnp.float32)
    end_logs = cumlog[:, :, -1]
    in_weights = jnp.exp(end_logs[:, :, None] - cumlog) * steps_here
    b_weighted = (b_rows[:, None].astype(jnp.float32) * in_weights[..., None]).astype(jnp.bfloat16)
    block_states = jnp.einsum(
        "cshp,chsn->chpn", blocks_x, b_weighted, preferred_element_type=jnp.float32
    )

    def advance(carried, inputs):
        gain_log, block_state = inputs
        return (jnp.exp(gain_log)[:, None, None] * carried + block_state, carried)

    initial = jnp.zeros(block_states.shape[1:], jnp.float32)
    end_state, entering = lax.scan(advance, initial, (end_logs, block_states))
    before = jnp.cumsum(end_logs, axis=0) - end_logs
    whole_decay = jnp.exp(jnp.sum(end_logs, axis=0))
    return ((intra_out, entering, cumlog, before, c_rows), (whole_decay, end_state))


def finish(pieces, carried):
    intra_out, entering, cumlog, before, c_rows = pieces
    states = entering + jnp.exp(before)[:, :, None, None] * carried[None]
    inter = jnp.einsum("ctn,chpn->cthp", c_rows.astype(jnp.float32), states)
    inter = inter * jnp.exp(cumlog).transpose(0, 2, 1)[..., None]
    outputs = intra_out + inter
    return outputs.reshape(outputs.shape[0] * outputs.shape[1], -1)


def body(
    ssm_input,
    gate_z,
    proj_forward,
    proj_backward,
    step_raw,
    head_params,
    skip_gain,
    norm_gain,
    out_weight,
):
    frames, inner_here = ssm_input.shape
    heads_here = step_raw.shape[1]
    width = inner_here // heads_here
    blocks = frames // SPAN
    shape_x = (blocks, SPAN, heads_here, width)
    shape_rows = (blocks, SPAN, proj_forward.shape[2])

    def to_blocks(steps):
        return steps.reshape(heads_here, blocks, SPAN).transpose(1, 0, 2)

    steps_fwd = jax.nn.softplus(step_raw[0] + head_params[0, 1][:, None])
    steps_bwd = jax.nn.softplus(step_raw[1] + head_params[1, 1][:, None])[:, ::-1]
    fwd_parts, fwd_end = local_scan(
        ssm_input.reshape(shape_x),
        proj_forward[0].reshape(shape_rows),
        proj_forward[1].reshape(shape_rows),
        to_blocks(steps_fwd),
        head_params[0, 0],
    )
    bwd_parts, bwd_end = local_scan(
        ssm_input[::-1].reshape(shape_x),
        proj_backward[0][::-1].reshape(shape_rows),
        proj_backward[1][::-1].reshape(shape_rows),
        to_blocks(steps_bwd),
        head_params[1, 0],
    )
    decays_all, states_all = tuple(
        (
            part.astype(jnp.float32)
            for part in sent_together(
                (
                    jnp.stack([fwd_end[0], bwd_end[0]])[None].astype(jnp.bfloat16),
                    jnp.stack([fwd_end[1], bwd_end[1]])[None].astype(jnp.bfloat16),
                ),
                "seq",
                0,
                3,
            )
        )
    )
    own_index = lax.axis_index("seq")
    group_size = lax.axis_size("seq")

    def accumulate(position, carried):
        forward_state, backward_state = carried
        mirror = group_size - 1 - position
        forward_state = jnp.where(
            position < own_index,
            decays_all[position, 0][:, None, None] * forward_state + states_all[position, 0],
            forward_state,
        )
        backward_state = jnp.where(
            mirror > own_index,
            decays_all[mirror, 1][:, None, None] * backward_state + states_all[mirror, 1],
            backward_state,
        )
        return (forward_state, backward_state)

    empty_state = jnp.zeros(fwd_end[1].shape, jnp.float32)
    carry_fwd, carry_bwd = lax.fori_loop(0, group_size, accumulate, (empty_state, empty_state))
    forward_out = finish(fwd_parts, carry_fwd)
    backward_out = finish(bwd_parts, carry_bwd)[::-1]
    skipped = (
        ssm_input.reshape(frames, heads_here, width).astype(jnp.float32) * skip_gain[:, None]
    ).reshape(frames, inner_here)
    gated = (forward_out + backward_out + skipped) * jax.nn.silu(gate_z.astype(jnp.float32))
    squares = taken_together(jnp.sum(gated * gated, axis=1), "chan")
    scale = lax.rsqrt(squares / INNER + 1.0)
    normed = (gated * scale[:, None] * norm_gain).astype(jnp.bfloat16)
    frame_share = lax.all_to_all(normed, "chan", split_axis=0, concat_axis=1, tiled=True)
    projected = jnp.dot(
        frame_share,
        lax.all_gather(out_weight, "chan", axis=1, tiled=True),
        preferred_element_type=jnp.float32,
    ).astype(jnp.bfloat16)
    return lax.all_to_all(projected, "chan", split_axis=1, concat_axis=0, tiled=True)


def solution(mesh):
    in_specs = (
        P(("batch", "seq"), "chan"),
        P(("batch", "seq"), "chan"),
        P(None, ("batch", "seq"), None),
        P(None, ("batch", "seq"), None),
        P(None, "chan", ("batch", "seq")),
        P(None, None, "chan"),
        P("chan"),
        P("chan"),
        P(None, "chan"),
    )
    out_specs = P(("batch", "seq"), "chan")
    return jax.shard_map(body, mesh=mesh, in_specs=in_specs, out_specs=out_specs, check_vma=False)
```

profile of v0, /device:TPU:96, one launch (start us, length us, event | category | flops | bytes accessed | tf_op | source)
XLA Modules:
  0.0 171.4 jit_solution(11320585137728651989)
XLA Ops:
  7.3 1.2 copy.167
  8.5 6.3 %rev.17 = bf16[1024,256]{1,0:T(8,128)(2,1)S(1)} reverse(bf16[1024,256]{1,0:T(8,128)(2,1)} %param.15), dimensions={0} | reverse | bytes 1048576 | tf_op jit(solution)/shard_map/rev | solution.py:97
  16.4 0.8 compare_select_fusion
  18.0 4.8 %reduce-window.14 = f32[4,4,2,128]{3,2,1,0:T(2,128)S(1)} reduce-window(f32[4,4,2,128]{3,2,1,0:T(2,128)S(1)} %reshape.296, f32[]{:T(128)} %constant.83.clone.1), window={size=1x1x1x128 pad=0_0x0_0x0_0x127_0}, to_apply=%region_0.1 | reduce-window | flops 520192 | bytes 32772 | tf_op jit(solution)/shard_map/reduce-window
  23.6 1.1 fusion.56
  24.8 1.2 reshape.298
  26.6 1.9 %convolution_bitcast_fusion.3 = f32[4,4,64,128]{3,2,1,0:T(8,128)S(1)} fusion(f32[4,4,256]{2,1,0:T(4,128)S(1)} %get-tuple-element.329, f32[4,256,128]{2,1,0:T(8,128)S(1)} %convert_element_type.76, bf16[4,256,4,64]{1,0,3,2:T(4,128)(2,1)} %reshape.298), kind=kOutput, calls=%fused_computation.48 | convolution fusion | flops 68157440 | bytes 1589248 | tf_op jit(solution)/shard_map/cshp,chsn->chpn/dot_general | solution.py:42
  29.3 4.8 %reduce-window.16 = f32[4,4,2,128]{3,2,1,0:T(2,128)S(1)} reduce-window(f32[4,4,2,128]{3,2,1,0:T(2,128)S(1)} %reshape.300, f32[]{:T(128)} %constant.83.clone.1), window={size=1x1x1x128 pad=0_0x0_0x0_0x127_0}, to_apply=%region_6.7 | reduce-window | flops 520192 | bytes 32772 | tf_op jit(solution)/shard_map/reduce-window.2
  34.9 1.8 %slice_bitcast_fusion = (bf16[1024,128]{1,0:T(8,128)(2,1)}, bf16[1024,128]{1,0:T(8,128)(2,1)S(1)}) fusion(bf16[2,1024,128]{2,1,0:T(8,128)(2,1)} %param.18), kind=kLoop, calls=%fused_computation.70 | loop fusion | bytes 1048576 | tf_op jit(solution)/shard_map/squeeze | solution.py:99
  36.9 0.8 convert_element_type.78
  39.3 2.0 %convolution_bitcast_fusion.2 = f32[4,4,64,128]{3,2,1,0:T(8,128)S(1)} fusion(bf16[4,256,4,64]{1,3,2,0:T(8,128)(2,1)S(1)} %copy.176, f32[4,4,256]{2,1,0:T(4,128)S(1)} %get-tuple-element.324, f32[4,256,128]{2,1,0:T(8,128)} %convert_element_type.78), kind=kOutput, calls=%fused_computation.47 | convolution fusion | flops 68157440 | bytes 1589248 | tf_op jit(solution)/shard_map/cshp,chsn->chpn/dot_general | solution.py:42
  42.7 2.0 %all_gather.6 = bf16[2,2,4,8193]{3,2,1,0:T(4,128)(2,1)S(1)} all-gather(bf16[1,2,4,8193]{3,2,1,0:T(4,128)(2,1)S(1)} %maximum_maximum_fusion), channel_id=1, replica_groups=mesh['seq'=2,'chan'=16,'batch'=8] {'seq'}, dimensions={0}, use_global_device_ids=true | all-gather | bytes 393264 | tf_op jit(solution)/shard_map/all_gather | solution.py:13
  45.4 3.2 %rev.18 = bf16[1024,128]{1,0:T(8,128)(2,1)S(1)} reverse(bf16[1024,128]{1,0:T(8,128)(2,1)} %get-tuple-element.319), dimensions={0} | reverse | bytes 524288 | tf_op jit(solution)/shard_map/rev | solution.py:99
  49.6 3.1 %fusion.22 = f32[4,256,4,64]{1,3,2,0:T(8,128)} fusion(bf16[4,256,4,64]{1,3,2,0:T(8,128)(2,1)S(1)} %copy.176, f32[4,4,256]{2,1,0:T(4,128)} %bitcast.166, f32[4,4,256]{2,1,0:T(4,128)S(1)} %copy-done.9, f32[4,256,256]{2,1,0:T(8,128)S(1)} %fusion.58, pred[256,256]{1,0:T(8,128)(4,1)S(1)} %iota_compare_fusion), kind=kOutput, calls=%fused_computation.37 | convolution fusion | flops 140509184 | bytes 2719744 | tf_op jit(solution)/shard_map/chts,cshp->cthp/dot_general | solution.py:38
  53.8 1.6 fusion.25
  56.3 1.5 rev.19
  58.2 2.5 %fusion.23 = f32[4,256,4,64]{1,3,2,0:T(8,128)S(1)} fusion(f32[4,4,256]{2,1,0:T(4,128)S(1)} %copy-done.13, f32[4,4,256]{2,1,0:T(4,128)S(1)} %copy-done.7, f32[4,256,256]{2,1,0:T(8,128)S(1)} %fusion.57, pred[256,256]{1,0:T(8,128)(4,1)S(1)} %copy-done.11, bf16[4,256,4,64]{1,0,3,2:T(4,128)(2,1)} %reshape.298), kind=kOutput, calls=%fused_computation.38 | convolution fusion | flops 140509184 | bytes 2719744 | tf_op jit(solution)/shard_map/chts,cshp->cthp/dot_general | solution.py:38
  61.8 1.2 copy.198
  63.3 1.8 %multiply_reduce_fusion = (f32[1024]{0:T(1024)S(1)}, f32[1024,256]{0,1:T(8,128)S(1)}) fusion(bf16[1024,256]{0,1:T(8,128)(2,1)S(1)} %copy.182, f32[256]{0:T(256)S(1)} %mul.274, bf16[1024,256]{0,1:T(8,128)(2,1)S(1)} %copy.167, f32[1024,256]{0,1:T(8,128)} %bitcast.150, f32[1024,256]{0,1:T(8,128)S(1)} %rev.19), kind=kLoop, calls=%fused_computation.55 | loop fusion | flops 3144704 | bytes 4199424 | tf_op jit(solution)/shard_map/reduce_sum | solution.py:143
  65.2 15.2 %all_to_all.46 = f32[16,1,1024]{2,1,0:T(1,128)S(1)} all-to-all(f32[16,1,1024]{2,1,0:T(1,128)S(1)} %broadcast_in_dim.57), channel_id=1, replica_groups=mesh['seq'=2,'chan'=16,'batch'=8] {'chan'}, dimensions={0} | all-to-all | bytes 131072 | tf_op jit(solution)/shard_map/all_to_all | solution.py:23
  80.8 18.8 %all_to_all.44 = bf16[16,64,256]{2,1,0:T(8,128)(2,1)S(1)} all-to-all(bf16[16,64,256]{2,1,0:T(8,128)(2,1)S(1)} %bitcast.160), channel_id=1, replica_groups=mesh['seq'=2,'chan'=16,'batch'=8] {'chan'}, dimensions={0} | all-to-all | bytes 1048576 | tf_op jit(solution)/shard_map/all_to_all | solution.py:146
  99.7 42.4 %all-gather.2.cloned.1.call-done = bf16[4096,2048]{1,0:T(8,128)(2,1)} async-done(((bf16[4096,128]{1,0:T(8,128)(2,1)}), bf16[4096,2048]{1,0:T(8,128)(2,1)}) %all-gather.2.cloned.1.call-update) | async-done | bytes 16777232 | tf_op jit(solution)/shard_map/all_gather | solution.py:149
  142.1 8.8 %fusion.28 = bf16[8,16,8,128]{3,2,1,0:T(8,128)(2,1)S(1)} fusion(bf16[64,4096]{1,0:T(8,128)(2,1)S(1)} %bitcast.151, bf16[4096,2048]{1,0:T(8,128)(2,1)} %all-gather.2.cloned.1.call-done), kind=kOutput, calls=%fused_computation.49 | convolution fusion | flops 1073872896 | bytes 17563648 | tf_op jit(solution)/shard_map/dot_general | solution.py:147
  150.9 12.9 %all_to_all.45 = bf16[64,16,128]{2,0,1:T(8,128)(2,1)S(1)} all-to-all(bf16[64,16,128]{2,0,1:T(8,128)(2,1)S(1)} %bitcast.162), channel_id=1, replica_groups=mesh['seq'=2,'chan'=16,'batch'=8] {'chan'}, dimensions={1} | all-to-all | bytes 524288 | tf_op jit(solution)/shard_map/all_to_all | solution.py:152
  (143 shorter events, 16.7 us)
Async XLA Ops:
  6.5 135.5 %all-gather.2.cloned.1.call-start = ((), (), s32[]{:S(2)}) async-start(), calls=%async_computation.3 | async-start | bytes 17825792 | tf_op jit(solution)/shard_map/all_gather | solution.py:149
  17.9 20.8 %copy-start.5 = (f32[4,1024]{1,0:T(4,128)}, f32[4,1024]{1,0:T(4,128)S(1)}, u32[]{:S(2)}) copy-start(f32[4,1024]{1,0:T(4,128)S(1)} %rev.15) | copy-start | bytes 49156
  18.0 10.6 %copy-start.12 = (f32[4,4,256]{2,1,0:T(4,128)}, f32[4,4,256]{2,1,0:T(4,128)S(1)}, u32[]{:S(2)}) copy-start(f32[4,4,256]{2,1,0:T(4,128)S(1)} %get-tuple-element.314) | copy-start | bytes 49156
  23.3 3.3 %copy-start.6 = (f32[4,4,256]{2,1,0:T(4,128)}, f32[4,4,256]{2,1,0:T(4,128)S(1)}, u32[]{:S(2)}) copy-start(f32[4,4,256]{2,1,0:T(4,128)S(1)} %reduce_window_sum.59) | copy-start | bytes 49156
  29.2 7.5 %copy-start = (f32[4,4,64,128]{3,2,1,0:T(8,128)}, f32[4,4,64,128]{3,2,1,0:T(8,128)S(1)}, u32[]{:S(2)}) copy-start(f32[4,4,64,128]{3,2,1,0:T(8,128)S(1)} %get-tuple-element.216) | copy-start | bytes 1572868
  29.2 7.7 %copy-start.16 = (f32[4,4]{1,0:T(4,128)}, f32[4,4]{1,0:T(4,128)S(1)}, u32[]{:S(2)}) copy-start(f32[4,4]{1,0:T(4,128)S(1)} %get-tuple-element.516) | copy-start | bytes 196
  34.6 6.8 %copy-start.8 = (f32[4,4,256]{2,1,0:T(4,128)}, f32[4,4,256]{2,1,0:T(4,128)S(1)}, u32[]{:S(2)}) copy-start(f32[4,4,256]{2,1,0:T(4,128)S(1)} %reduce_window_sum.62) | copy-start | bytes 49156
  42.0 0.8 copy-start.2
  42.0 7.6 %copy-start.9 = (f32[4,4,256]{2,1,0:T(4,128)S(1)}, f32[4,4,256]{2,1,0:T(4,128)}, u32[]{:S(2)}) copy-start(f32[4,4,256]{2,1,0:T(4,128)} %copy-done.8) | copy-start | bytes 49156
  48.7 4.1 %copy-start.10 = (pred[256,256]{1,0:T(8,128)(4,1)}, pred[256,256]{1,0:T(8,128)(4,1)S(1)}, u32[]{:S(2)}) copy-start(pred[256,256]{1,0:T(8,128)(4,1)S(1)} %iota_compare_fusion) | copy-start | bytes 196612
  52.7 1.0 copy-start.3
  52.7 1.0 copy-start.15
  55.3 2.4 %copy-start.17 = (f32[4,4]{1,0:T(4,128)S(1)}, f32[4,4]{1,0:T(4,128)}, u32[]{:S(2)}) copy-start(f32[4,4]{1,0:T(4,128)} %copy-done.16) | copy-start | bytes 196
  55.3 2.8 %copy-start.7 = (f32[4,4,256]{2,1,0:T(4,128)S(1)}, f32[4,4,256]{2,1,0:T(4,128)}, u32[]{:S(2)}) copy-start(f32[4,4,256]{2,1,0:T(4,128)} %copy-done.6) | copy-start | bytes 49156
  55.4 2.8 %copy-start.11 = (pred[256,256]{1,0:T(8,128)(4,1)S(1)}, pred[256,256]{1,0:T(8,128)(4,1)}, u32[]{:S(2)}) copy-start(pred[256,256]{1,0:T(8,128)(4,1)} %copy-done.10) | copy-start | bytes 196612
  55.4 2.8 %copy-start.13 = (f32[4,4,256]{2,1,0:T(4,128)S(1)}, f32[4,4,256]{2,1,0:T(4,128)}, u32[]{:S(2)}) copy-start(f32[4,4,256]{2,1,0:T(4,128)} %copy-done.12) | copy-start | bytes 49156
  58.2 2.5 %copy-start.1 = (f32[4,4,64,128]{3,2,1,0:T(8,128)S(1)}, f32[4,4,64,128]{3,2,1,0:T(8,128)}, u32[]{:S(2)}) copy-start(f32[4,4,64,128]{3,2,1,0:T(8,128)} %copy-done) | copy-start | bytes 1572868
  58.2 2.5 %copy-start.14 = (f32[4,256,4]{1,2,0:T(4,128)S(1)}, f32[4,256,4]{1,2,0:T(4,128)}, u32[]{:S(2)}) copy-start(f32[4,256,4]{1,2,0:T(4,128)} %get-tuple-element.330) | copy-start | bytes 49156
  60.7 2.3 %copy-start.4 = (bf16[1024,256]{1,0:T(8,128)(2,1)S(1)}, bf16[1024,256]{1,0:T(8,128)(2,1)}, u32[]{:S(2)}) copy-start(bf16[1024,256]{1,0:T(8,128)(2,1)} %param.16) | copy-start | bytes 1572868
  60.7 2.5 %copy-start.19 = (f32[4]{0:T(128)S(1)}, f32[4]{0:T(128)}, u32[]{:S(2)}) copy-start(f32[4]{0:T(128)} %param.21) | copy-start | bytes 52
  61.8 18.7 %copy-start.18 = (f32[256]{0:T(256)S(1)}, f32[256]{0:T(256)}, u32[]{:S(2)}) copy-start(f32[256]{0:T(256)} %param.22) | copy-start | bytes 3076
Sparse Core Ops, SparseCore 0:
  9.7 132.2 all-gather.1
where the time goes:
time: 173 us; the launch traced here: 171 us
  blocking collectives  48.9 us (28%)
  waiting for transfers between devices  43.1 us (25%)
  local copies, waits for them, and re-layouts  26 us (15%)
  matrix products  20.8 us (12%)
  other arithmetic  18.2 us (11%)
  between operations  14 us (8%)
    all_gather x1, waiting for transfers between devices, body(): lax.all_gather(out_weight, 'chan', axis=1, tiled=True)  42.4 us
    all_to_all x1, blocking collectives, body(): lax.all_to_all(normed, 'chan', split_axis=0, concat_axis=1, tiled=True)  18.8 us
    all_to_all x1, blocking collectives, copy_for_each(): return lax.all_to_all(copies, axis, split_axis=0, concat_axis=0, tiled=True)  15.2 us
    all_to_all x1, blocking collectives, body(): lax.all_to_all(projected, 'chan', split_axis=1, concat_axis=0, tiled=True)  12.9 us
    another operation x8, other arithmetic  9.88 us
    dot_general x1, matrix products, body(): jnp.dot(frame_share, lax.all_gather(out_weight, 'chan', axis=1, tiled=Tru...  8.79 us
    rev x1, local copies, waits for them, and re-layouts, body(): ssm_input[::-1].reshape(shape_x)  6.33 us
    dot_general x2, matrix products, local_scan(): jnp.einsum('chts,cshp->cthp', weights, blocks_x, preferred_element_type=j...  5.62 us
  transfers between devices with their start and end apart: 1, of which 1 were waited for; matrix products, arithmetic and copies ran while one was open for 32% of the time, Pallas kernels for 0%

commit v1 on v0

--- a/solution.py
+++ b/solution.py
@@ -5,6 +5,7 @@
 
 SPAN = 256
 INNER = 4096
+slabs_replace = lambda x0, net_axis: jnp.concatenate(lax.all_gather(x0, axis_name=net_axis), axis=1)
 
 
 def sent_together(arrays, axis, dim, along):
@@ -145,9 +146,7 @@
     normed = (gated * scale[:, None] * norm_gain).astype(jnp.bfloat16)
     frame_share = lax.all_to_all(normed, "chan", split_axis=0, concat_axis=1, tiled=True)
     projected = jnp.dot(
-        frame_share,
-        lax.all_gather(out_weight, "chan", axis=1, tiled=True),
-        preferred_element_type=jnp.float32,
+        frame_share, slabs_replace(out_weight, "chan"), preferred_element_type=jnp.float32
     ).astype(jnp.bfloat16)
     return lax.all_to_all(projected, "chan", split_axis=1, concat_axis=0, tiled=True)
 

time: 173 us -> 190 us (1.098)
  local copies, waits for them, and re-layouts: 26 us -> 43.3 us
  waiting for transfers between devices: 43.1 us -> 37.8 us
  blocking collectives: 48.9 us -> 52 us
    reshape x1 -> x2, local copies, waits for them, and re-layouts: 0.02 us -> 20.8 us  [the longest x1 20.8 us: jnp.concatenate(lax.all_gather(x0, axis_name=net_axis), axis=1)]
    all_gather x1, waiting for transfers between devices: 42.4 us -> 37.1 us  [lax.all_gather(x0, axis_name=net_axis)]
    rev x1, local copies, waits for them, and re-layouts: 3.17 us -> 0.28 us  [body(): proj_backward[1][::-1].reshape(shape_rows)]
    dot_general x1, matrix products: 8.79 us -> 11 us  [body(): jnp.dot(frame_share, slabs_replace(out_weight, 'chan'), preferred_element...]
    all_to_all x1, blocking collectives: 18.8 us -> 20.8 us  [body(): lax.all_to_all(normed, 'chan', split_axis=0, concat_axis=1, tiled=True)]
    unnamed x47 -> x37, local copies, waits for them, and re-layouts: 4.97 us -> 4.15 us
  transfers between devices with their start and end apart: 1 -> 1, of which waited for: 1 -> 1; matrix products, arithmetic and copies ran while one was open for 32% -> 27% of each run, Pallas kernels for 0% -> 0%
where the time goes in v1:
time: 190 us; the launch traced here: 187 us
  blocking collectives  52 us (27%)
  local copies, waits for them, and re-layouts  43.3 us (23%)
  waiting for transfers between devices  37.8 us (20%)
  matrix products  21.3 us (11%)
  other arithmetic  18.5 us (10%)
  between operations  13.9 us (7%)
    all_gather x1, waiting for transfers between devices, lax.all_gather(x0, axis_name=net_axis)  37.1 us
    all_to_all x1, blocking collectives, body(): lax.all_to_all(normed, 'chan', split_axis=0, concat_axis=1, tiled=True)  20.8 us
    reshape x1, local copies, waits for them, and re-layouts, jnp.concatenate(lax.all_gather(x0, axis_name=net_axis), axis=1)  20.8 us
    all_to_all x1, blocking collectives, copy_for_each(): return lax.all_to_all(copies, axis, split_axis=0, concat_axis=0, tiled=True)  15.3 us
    all_to_all x1, blocking collectives, body(): lax.all_to_all(projected, 'chan', split_axis=1, concat_axis=0, tiled=True)  13.7 us
    dot_general x1, matrix products, body(): jnp.dot(frame_share, slabs_replace(out_weight, 'chan'), preferred_element...  11 us
    another operation x8, other arithmetic  9.89 us
    rev x1, local copies, waits for them, and re-layouts, body(): ssm_input[::-1].reshape(shape_x)  6.33 us
  transfers between devices with their start and end apart: 1, of which 1 were waited for; matrix products, arithmetic and copies ran while one was open for 27% of the time, Pallas kernels for 0%

profile of v1, /device:TPU:96, one launch (start us, length us, event | category | flops | bytes accessed | tf_op | source)
XLA Modules:
  0.0 187.3 jit_solution(7060594338572278767)
XLA Ops:
  7.3 1.3 copy.172
  8.6 6.3 %rev.17 = bf16[1024,256]{1,0:T(8,128)(2,1)S(1)} reverse(bf16[1024,256]{1,0:T(8,128)(2,1)} %param.15), dimensions={0} | reverse | bytes 1048576 | tf_op jit(solution)/shard_map/rev | solution.py:98
  17.1 0.8 negate_bitcast_fusion
  17.8 0.8 compare_select_fusion
  19.5 4.8 %reduce-window.14 = f32[4,4,2,128]{3,2,1,0:T(2,128)S(1)} reduce-window(f32[4,4,2,128]{3,2,1,0:T(2,128)S(1)} %reshape.302, f32[]{:T(128)} %constant.83.clone.1), window={size=1x1x1x128 pad=0_0x0_0x0_0x127_0}, to_apply=%region_0.1 | reduce-window | flops 520192 | bytes 32772 | tf_op jit(solution)/shard_map/reduce-window
  25.1 4.8 %reduce-window.16 = f32[4,4,2,128]{3,2,1,0:T(2,128)S(1)} reduce-window(f32[4,4,2,128]{3,2,1,0:T(2,128)S(1)} %reshape.306, f32[]{:T(128)} %constant.83.clone.1), window={size=1x1x1x128 pad=0_0x0_0x0_0x127_0}, to_apply=%region_6.7 | reduce-window | flops 520192 | bytes 32772 | tf_op jit(solution)/shard_map/reduce-window.2
  30.8 1.2 reshape.304
  32.0 1.0 copy.187
  35.5 1.8 convolution_bitcast_fusion.3
  38.1 1.2 slice_bitcast_fusion
  41.2 1.0 convolution_bitcast_fusion.2
  43.0 2.1 %all_gather.9 = bf16[2,2,4,8193]{3,2,1,0:T(4,128)(2,1)} all-gather(bf16[1,2,4,8193]{3,2,1,0:T(4,128)(2,1)S(1)} %maximum_maximum_fusion), channel_id=1, replica_groups=mesh['seq'=2,'chan'=16,'batch'=8] {'seq'}, dimensions={0}, use_global_device_ids=true | all-gather | bytes 393264 | tf_op jit(solution)/shard_map/all_gather | solution.py:14
  45.2 1.2 slice_convert_fusion
  46.7 0.8 convert_reduce_fusion
  48.5 2.5 %fusion.22 = f32[4,256,4,64]{1,3,2,0:T(8,128)} fusion(bf16[4,256,4,64]{1,3,2,0:T(8,128)(2,1)S(1)} %copy.181, f32[4,4,256]{2,1,0:T(4,128)S(1)} %bitcast.172, f32[4,4,256]{2,1,0:T(4,128)S(1)} %reduce_window_sum.62, f32[4,256,256]{2,1,0:T(8,128)S(1)} %fusion.58, pred[256,256]{1,0:T(8,128)(4,1)S(1)} %iota_compare_fusion), kind=kOutput, calls=%fused_computation.37 | convolution fusion | flops 140509184 | bytes 2719744 | tf_op jit(solution)/shard_map/chts,cshp->cthp/dot_general | solution.py:39
  51.7 1.6 fusion.25
  54.2 1.5 rev.19
  56.0 2.5 %fusion.23 = f32[4,256,4,64]{1,3,2,0:T(8,128)S(1)} fusion(f32[4,4,256]{2,1,0:T(4,128)S(1)} %get-tuple-element.314, f32[4,4,256]{2,1,0:T(4,128)S(1)} %reduce_window_sum.59, f32[4,256,256]{2,1,0:T(8,128)S(1)} %fusion.57, pred[256,256]{1,0:T(8,128)(4,1)S(1)} %iota_compare_fusion, bf16[4,256,4,64]{1,0,3,2:T(4,128)(2,1)} %reshape.304), kind=kOutput, calls=%fused_computation.38 | convolution fusion | flops 140509184 | bytes 2719744 | tf_op jit(solution)/shard_map/chts,cshp->cthp/dot_general | solution.py:39
  60.5 15.3 %all_to_all.46 = f32[16,1,1024]{2,1,0:T(1,128)S(1)} all-to-all(f32[16,1,1024]{2,1,0:T(1,128)S(1)} %broadcast_in_dim.57), channel_id=1, replica_groups=mesh['seq'=2,'chan'=16,'batch'=8] {'chan'}, dimensions={0} | all-to-all | bytes 131072 | tf_op jit(solution)/shard_map/all_to_all | solution.py:24
  76.2 20.8 %all_to_all.44 = bf16[16,64,256]{2,1,0:T(8,128)(2,1)S(1)} all-to-all(bf16[16,64,256]{2,1,0:T(8,128)(2,1)S(1)} %bitcast.166), channel_id=1, replica_groups=mesh['seq'=2,'chan'=16,'batch'=8] {'chan'}, dimensions={0} | all-to-all | bytes 1048576 | tf_op jit(solution)/shard_map/all_to_all | solution.py:147
  97.1 37.1 %all-gather.3.cloned.1.call-done = bf16[65536,128]{1,0:T(8,128)(2,1)} async-done(((bf16[4096,128]{1,0:T(8,128)(2,1)}), bf16[65536,128]{1,0:T(8,128)(2,1)}) %all-gather.3.cloned.1.call-update) | async-done | bytes 16777232 | tf_op jit(solution)/shard_map/all_gather | solution.py:8
  134.2 20.8 %copy.191 = bf16[4096,16,128]{0,2,1:T(8,128)(2,1)} copy(bf16[4096,16,128]{2,0,1:T(8,128)(2,1)} %bitcast.152) | data formatting | bytes 33554432 | tf_op jit(solution)/shard_map/reshape | solution.py:8
  155.0 11.0 %fusion.28 = bf16[8,16,8,128]{3,2,1,0:T(8,128)(2,1)S(1)} fusion(bf16[64,4096]{1,0:T(8,128)(2,1)S(1)} %bitcast.165, bf16[4096,2048]{0,1:T(8,128)(2,1)} %bitcast.151), kind=kOutput, calls=%fused_computation.49 | convolution fusion | flops 1073872896 | bytes 17563648 | tf_op jit(solution)/shard_map/dot_general | solution.py:148
  166.0 13.7 %all_to_all.45 = bf16[64,16,128]{2,0,1:T(8,128)(2,1)S(1)} all-to-all(bf16[64,16,128]{2,0,1:T(8,128)(2,1)S(1)} %bitcast.168), channel_id=1, replica_groups=mesh['seq'=2,'chan'=16,'batch'=8] {'chan'}, dimensions={1} | all-to-all | bytes 524288 | tf_op jit(solution)/shard_map/all_to_all | solution.py:151
  (134 shorter events, 18.5 us)
Async XLA Ops:
  6.5 25.5 %copy-start.6 = (bf16[1024,256]{1,0:T(8,128)(2,1)S(1)}, bf16[1024,256]{1,0:T(8,128)(2,1)}, u32[]{:S(2)}) copy-start(bf16[1024,256]{1,0:T(8,128)(2,1)} %param.16) | copy-start | bytes 1572868
  6.5 127.7 %all-gather.3.cloned.1.call-start = ((), (), s32[]{:S(2)}) async-start(), calls=%async_computation.3 | async-start | bytes 17825792 | tf_op jit(solution)/shard_map/all_gather | solution.py:8
  7.3 26.8 %copy-start.7 = (bf16[2,1024,128]{2,1,0:T(8,128)(2,1)S(1)}, bf16[2,1024,128]{2,1,0:T(8,128)(2,1)}, u32[]{:S(2)}) copy-start(bf16[2,1024,128]{2,1,0:T(8,128)(2,1)} %param.17) | copy-start | bytes 1572868
  34.8 5.1 %copy-start = (bf16[1,1024,128]{2,1,0:T(8,128)(2,1)}, bf16[1,1024,128]{2,1,0:T(8,128)(2,1)S(1)}, u32[]{:S(2)}) copy-start(bf16[1,1024,128]{2,1,0:T(8,128)(2,1)S(1)} %get-tuple-element.321) | copy-start | bytes 786436
  38.0 3.1 %copy-start.3 = (f32[4,4,64,128]{3,2,1,0:T(8,128)}, f32[4,4,64,128]{3,2,1,0:T(8,128)S(1)}, u32[]{:S(2)}) copy-start(f32[4,4,64,128]{3,2,1,0:T(8,128)S(1)} %get-tuple-element.216) | copy-start | bytes 1572868
  38.0 4.2 %copy-start.9 = (f32[4,4]{1,0:T(4,128)}, f32[4,4]{1,0:T(4,128)S(1)}, u32[]{:S(2)}) copy-start(f32[4,4]{1,0:T(4,128)S(1)} %get-tuple-element.516) | copy-start | bytes 196
  42.8 3.9 %copy-start.11 = (f32[4,4]{1,0:T(4,128)}, f32[4,4]{1,0:T(4,128)S(1)}, u32[]{:S(2)}) copy-start(f32[4,4]{1,0:T(4,128)S(1)} %get-tuple-element.517) | copy-start | bytes 196
  50.9 0.7 copy-start.8
  51.6 4.0 %copy-start.10 = (f32[4,4]{1,0:T(4,128)S(1)}, f32[4,4]{1,0:T(4,128)}, u32[]{:S(2)}) copy-start(f32[4,4]{1,0:T(4,128)} %copy-done.9) | copy-start | bytes 196
  51.6 4.1 %copy-start.12 = (f32[4,4]{1,0:T(4,128)S(1)}, f32[4,4]{1,0:T(4,128)}, u32[]{:S(2)}) copy-start(f32[4,4]{1,0:T(4,128)} %reduce_window_sum.60) | copy-start | bytes 196
  51.6 4.1 %copy-start.1 = (bf16[1,1024,128]{2,1,0:T(8,128)(2,1)S(1)}, bf16[1,1024,128]{2,1,0:T(8,128)(2,1)}, u32[]{:S(2)}) copy-start(bf16[1,1024,128]{2,1,0:T(8,128)(2,1)} %copy-done) | copy-start | bytes 786436
  51.6 4.1 %copy-start.2 = (bf16[1,1024,128]{2,1,0:T(8,128)(2,1)S(1)}, bf16[1,1024,128]{2,1,0:T(8,128)(2,1)}, u32[]{:S(2)}) copy-start(bf16[1,1024,128]{2,1,0:T(8,128)(2,1)} %get-tuple-element.322) | copy-start | bytes 786436
  56.0 2.5 %copy-start.4 = (f32[4,4,64,128]{3,2,1,0:T(8,128)S(1)}, f32[4,4,64,128]{3,2,1,0:T(8,128)}, u32[]{:S(2)}) copy-start(f32[4,4,64,128]{3,2,1,0:T(8,128)} %copy-done.3) | copy-start | bytes 1572868
  58.5 1.3 copy-start.5
  58.5 1.3 copy-start.13
  58.9 17.0 %copy-start.14 = (f32[256]{0:T(256)S(1)}, f32[256]{0:T(256)}, u32[]{:S(2)}) copy-start(f32[256]{0:T(256)} %param.22) | copy-start | bytes 3076
Sparse Core Ops, SparseCore 0:
  9.8 124.4 all-gather.2
